TPU v7x, 32 devices: a whole 2x2x4 slice. The times are simulated.
32 devices in a mesh: year: 8 (over y, x, core), port: 4 (over z).
Axes of the slice: x: 2, y: 2, z: 4, core: 2. Of those that a mesh axis runs over, the one named last changes fastest.
Arguments:
- event_loss: bfloat16 [4096, 4096], P('year', 'port'), may hold values from 0 to 24
- event_year: int32 [4096], P('year'), may hold values from -1 to 255, as said below
- retention: float32 [4096], P('port'), may hold values from 0.2 to 2
- risk_limit: float32 [4096], P('port'), may hold values from 1 to 8
- cession_share: bfloat16 [4096, 4], P('port'), may hold values from 0.099609375 to 1
- member_treaty: int32 [4096, 4], P('port'), may hold values from 0 to 1023, all different within a row
- attach_tier: int32 [1024], P('port'), may hold values from 2 to 11
- limit_tier: int32 [1024], P('port'), may hold values from 2 to 10
- reinstatements: int32 [1024], P('port'), may hold values from 0 to 3
- reinstate_rate: float32 [1024], P('port'), may hold values from 0.1 to 1
- stop_attach: float32 [1024], P('port'), may hold values from 0.7 to 2
- stop_width: float32 [1024], P('port'), may hold values from 0.3 to 2
Outputs:
- layer_net: float32 [1024, 256], P('port', 'year')
- stop_loss: float32 [1024, 256], P('port', 'year')
- tail_mean: float32 [1024], P('port')
Inputs may be any that keep to these rules, and one draw needn't show every extreme that they name: `event_year`: the 512 rows of year-block b name years b * 32 to (b + 1) * 32 - 1 in nondecreasing order, followed by padding rows marked -1; at least one block has no padding row. `member_treaty`: each portfolio names 4 different treaties, and every treaty is named by some portfolio.
All inputs are finite; a program needn't handle non-finite values.
Results may differ from a plain program's by a relative error of at most 0.029.
Values may be sent and summed in bfloat16 or wider, within the bound.
A program may use at most 64 MiB of HBM per device.

v0:
```python
import jax
import jax.numpy as jnp
from jax import lax
from jax.sharding import PartitionSpec as P

TREATIES = 1024
MEMB = 4
YEAR_DEV = 32
TAIL = 16
UNIT_LOSS = 1.0


def combined_all(part, axis, combine):
    gathered = lax.all_gather(part, axis)

    def take(source):
        return lax.dynamic_index_in_dim(gathered, source, 0, False)

    return lax.fori_loop(
        1, lax.axis_size(axis), lambda source, state: combine(state, take(source)), take(0)
    )


def clamp_between(values, lower, upper):
    return jnp.minimum(jnp.maximum(values, lower), upper)


def top_years(values, keep_count):
    return jnp.sort(values, axis=1)[:, values.shape[1] - keep_count :]


def on_device(
    event_loss,
    event_year,
    retention,
    risk_limit,
    cession_share,
    member_treaty,
    attach_tier,
    limit_tier,
    reinstatements,
    reinstate_rate,
    stop_attach,
    stop_width,
):
    own_count = attach_tier.shape[0]
    ceded_loss = clamp_between(
        event_loss.astype(jnp.float32) - retention[None, :], 0.0, risk_limit[None, :]
    ).astype(jnp.bfloat16)
    treaty_ids = lax.broadcasted_iota(jnp.int32, (1, TREATIES), 1)
    weights = jnp.zeros((event_loss.shape[1], TREATIES), jnp.float32)
    for member_slot in range(MEMB):
        picked = member_treaty[:, member_slot : member_slot + 1] == treaty_ids
        weights = weights + jnp.where(
            picked, cession_share[:, member_slot : member_slot + 1].astype(jnp.float32), 0.0
        )
    weights = weights.astype(jnp.bfloat16)
    first_year = lax.axis_index("year") * YEAR_DEV
    local_year = event_year - first_year
    contract = (((0,), (1,)), ((), ()))
    event_treaty = lax.psum_scatter(
        lax.dot_general(weights, ceded_loss, contract, preferred_element_type=jnp.float32).astype(
            jnp.bfloat16
        ),
        "port",
        scatter_dimension=0,
        tiled=True,
    ).astype(jnp.float32)
    attach = attach_tier.astype(jnp.float32) * UNIT_LOSS
    limit_loss = limit_tier.astype(jnp.float32) * UNIT_LOSS
    recovered = clamp_between(event_treaty - attach[:, None], 0.0, limit_loss[:, None])
    retained = event_treaty - recovered
    year_hits = (local_year[:, None] == lax.broadcasted_iota(jnp.int32, (1, YEAR_DEV), 1)).astype(
        jnp.float32
    )
    yearly = jnp.dot(
        jnp.concatenate((recovered, retained), 0),
        year_hits,
        precision=lax.Precision.HIGHEST,
        preferred_element_type=jnp.float32,
    )
    annual = yearly[:own_count]
    kept_annual = yearly[own_count:]
    reinstated = reinstatements.astype(jnp.float32)
    layer_paid = jnp.minimum(annual, ((1.0 + reinstated) * limit_loss)[:, None])
    layer_net = (
        layer_paid
        - reinstate_rate[:, None] * jnp.minimum(layer_paid, (reinstated * limit_loss)[:, None])
    ) / limit_loss[:, None]
    year_total = YEAR_DEV * lax.axis_size("year")
    summed = lax.psum(jnp.sum(kept_annual, axis=1), "year")
    base_loss = UNIT_LOSS + summed / year_total
    loss_ratio = kept_annual / base_loss[:, None]

    def keep_largest(earlier, later):
        return top_years(jnp.concatenate((earlier, later), 1), TAIL)

    largest = combined_all(top_years(loss_ratio, TAIL), "year", keep_largest)
    tail_mean = jnp.mean(largest, axis=1)
    stop_loss = clamp_between(loss_ratio - stop_attach[:, None], 0.0, stop_width[:, None])
    return (layer_net, stop_loss, tail_mean)


def solution(mesh):
    return jax.shard_map(
        on_device,
        mesh=mesh,
        in_specs=(
            P("year", "port"),
            P("year"),
            P("port"),
            P("port"),
            P("port", None),
            P("port", None),
            P("port"),
            P("port"),
            P("port"),
            P("port"),
            P("port"),
            P("port"),
        ),
        out_specs=(P("port", "year"), P("port", "year"), P("port")),
        check_vma=False,
    )
```

profile of v0, /device:TPU:0, one launch (start us, length us, event | category | flops | bytes accessed | tf_op | source)
XLA Modules:
  0.0 85.3 jit_solution(53839467080890265)
XLA Ops:
  7.2 0.0 reduce-scatter.2.cloned.1.call-start
  7.2 0.9 %fusion.23 = (s32[1024,1]{0,1:T(1,128)S(1)}, s32[1024,1]{0,1:T(1,128)S(1)}, s32[1024,1]{0,1:T(1,128)S(1)}, s32[1024,1]{0,1:T(1,128)S(1)}) fusion(s32[1024,4]{0,1:T(4,128)} %param.19), kind=kLoop, calls=%fused_computation.49 | loop fusion | bytes 32768 | tf_op jit(solution)/shard_map/slice | solution.py:53
  8.1 0.9 %slice_convert_fusion.3 = (f32[1024,1]{0,1:T(1,128)S(1)}, f32[1024,1]{0,1:T(1,128)S(1)}, f32[1024,1]{0,1:T(1,128)S(1)}, f32[1024,1]{0,1:T(1,128)S(1)}) fusion(bf16[1024,4]{0,1:T(4,128)(2,1)} %param.18), kind=kLoop, calls=%fused_computation.41 | loop fusion | flops 4096 | bytes 24576 | tf_op jit(solution)/shard_map/jit(_where)/broadcast_in_dim | solution.py:54
  9.0 5.4 %fusion.10 = bf16[1024,512]{1,0:T(8,128)(2,1)} fusion(f32[1024]{0:T(1024)S(1)} %bitcast.26, s32[1024]{0:T(1024)S(1)} %bitcast.22, f32[1024]{0:T(1024)S(1)} %bitcast.27, s32[1024]{0:T(1024)S(1)} %bitcast.23, f32[1024]{0:T(1024)S(1)} %bitcast.25, s32[1024]{0:T(1024)S(1)} %bitcast.21, f32[1024]{0:T(1024)S(1)} %bitcast.24, s32[1024]{0:T(1024)S(1)} %bitcast.20, ...), kind=kOutput, calls=%fused_computation.19 | convolution fusion | flops 1089994752 | bytes 2138112 | tf_op jit(solution)/shard_map/dot_general | solution.py:62
  14.4 0.0 copy-start
  14.4 0.0 copy-start.5
  14.4 0.0 copy-start.6
  14.4 0.0 copy-start.1
  14.4 0.0 reduce-scatter.2.cloned.1.call-update
  14.5 0.6 copy-done
  15.1 0.0 copy-done.5
  15.1 0.0 copy-done.6
  15.1 0.0 copy-done.1
  15.1 0.0 copy-start.2
  15.2 0.0 copy-start.3
  15.2 0.0 copy-start.4
  15.2 29.4 %reduce-scatter.2.cloned.1.call-done = bf16[256,512]{1,0:T(8,128)(2,1)} async-done(((bf16[1024,512]{1,0:T(8,128)(2,1)}), bf16[256,512]{1,0:T(8,128)(2,1)}) %reduce-scatter.2.cloned.1.call-update) | async-done | bytes 262160 | tf_op jit(solution)/shard_map/reduce_scatter | solution.py:61
  44.6 1.1 %fusion.19 = (f32[256,512]{1,0:T(8,128)S(1)}, f32[256,512]{1,0:T(8,128)S(1)}) fusion(bf16[256,512]{1,0:T(8,128)(2,1)} %reduce-scatter.2.cloned.1.call-done, f32[256]{0:T(256)S(1)} %convert_element_type.35, f32[256]{0:T(256)S(1)} %convert_element_type.34), kind=kLoop, calls=%fused_computation.30 | loop fusion | flops 655360 | bytes 1312768 | tf_op jit(solution)/shard_map/min | solution.py:25
  45.8 0.7 fusion.11
  46.5 13.2 %psum.7 = f32[256]{0:T(256)S(1)} all-reduce(f32[256]{0:T(256)S(1)} %slice_reduce_fusion), channel_id=1, replica_groups=mesh['year'=8,'port'=4] {'year'}, use_global_device_ids=true, to_apply=%region_2.3 | all-reduce | flops 256 | bytes 2048 | tf_op jit(solution)/shard_map/psum | solution.py:91
  59.7 0.0 copy-done.2
  59.7 0.0 copy-done.3
  59.7 0.0 copy-done.4
  59.7 0.6 maximum_minimum_fusion
  60.4 1.1 %sort.34 = (f32[256,32]{0,1:T(8,128)S(1)}, s32[256,32]{0,1:T(8,128)}) sort(f32[256,32]{0,1:T(8,128)S(1)} %get-tuple-element.107, s32[256,32]{0,1:T(8,128)S(1)} %iota.16), dimensions={1}, to_apply=%region_3.4 | sort | flops 106496 | bytes 131072 | tf_op jit(solution)/shard_map/jit(sort)/sort | solution.py:29
  61.5 8.3 %all-gather = f32[2048,16]{0,1:T(8,128)S(1)} all-gather(f32[256,16]{0,1:T(8,128)S(1)} %slice.54), channel_id=2, replica_groups=mesh['year'=8,'port'=4] {'year'}, dimensions={0}, use_global_device_ids=true | all-gather | bytes 147456 | tf_op jit(solution)/shard_map/all_gather | solution.py:14
  69.8 8.1 %while.15 = (s32[]{:T(128)}, f32[256,16]{0,1:T(8,128)S(1)}, f32[8,256,16]{1,0,2:T(8,128)S(1)}, s32[]{:T(128)}, s32[]{:T(128)}, /*index=5*/s32[]{:T(128)}) while((s32[]{:T(128)}, f32[256,16]{0,1:T(8,128)S(1)}, f32[8,256,16]{1,0,2:T(8,128)S(1)}, s32[]{:T(128)}, s32[]{:T(128)}, /*index=5*/s32[]{:T(128)}) %tuple.56), condition=%wide.region_6.7_spmd, body=%wide.region_4.6_spmd.sunk | while | flops 114693 | bytes 327795 | solution.py:19
  69.9 1.1 %sort.36 = (f32[256,32]{0,1:T(8,128)S(1)}, s32[256,32]{0,1:T(8,128)}) sort(f32[256,32]{0,1:T(8,128)S(1)} %pad_maximum_fusion.2, s32[256,32]{0,1:T(8,128)S(1)} %iota.18), dimensions={1}, to_apply=%region_5.5 | sort | flops 106496 | bytes 131072 | tf_op jit(solution)/shard_map/while/body/eval_jaxpr/jit(sort)/sort | solution.py:29
  71.0 1.1 %sort.36 = (f32[256,32]{0,1:T(8,128)S(1)}, s32[256,32]{0,1:T(8,128)}) sort(f32[256,32]{0,1:T(8,128)S(1)} %pad_maximum_fusion.2, s32[256,32]{0,1:T(8,128)S(1)} %iota.18), dimensions={1}, to_apply=%region_5.5 | sort | flops 106496 | bytes 131072 | tf_op jit(solution)/shard_map/while/body/eval_jaxpr/jit(sort)/sort | solution.py:29
  72.2 1.1 %sort.36 = (f32[256,32]{0,1:T(8,128)S(1)}, s32[256,32]{0,1:T(8,128)}) sort(f32[256,32]{0,1:T(8,128)S(1)} %pad_maximum_fusion.2, s32[256,32]{0,1:T(8,128)S(1)} %iota.18), dimensions={1}, to_apply=%region_5.5 | sort | flops 106496 | bytes 131072 | tf_op jit(solution)/shard_map/while/body/eval_jaxpr/jit(sort)/sort | solution.py:29
  73.3 1.1 %sort.36 = (f32[256,32]{0,1:T(8,128)S(1)}, s32[256,32]{0,1:T(8,128)}) sort(f32[256,32]{0,1:T(8,128)S(1)} %pad_maximum_fusion.2, s32[256,32]{0,1:T(8,128)S(1)} %iota.18), dimensions={1}, to_apply=%region_5.5 | sort | flops 106496 | bytes 131072 | tf_op jit(solution)/shard_map/while/body/eval_jaxpr/jit(sort)/sort | solution.py:29
  74.5 1.1 %sort.36 = (f32[256,32]{0,1:T(8,128)S(1)}, s32[256,32]{0,1:T(8,128)}) sort(f32[256,32]{0,1:T(8,128)S(1)} %pad_maximum_fusion.2, s32[256,32]{0,1:T(8,128)S(1)} %iota.18), dimensions={1}, to_apply=%region_5.5 | sort | flops 106496 | bytes 131072 | tf_op jit(solution)/shard_map/while/body/eval_jaxpr/jit(sort)/sort | solution.py:29
  75.6 1.1 %sort.36 = (f32[256,32]{0,1:T(8,128)S(1)}, s32[256,32]{0,1:T(8,128)}) sort(f32[256,32]{0,1:T(8,128)S(1)} %pad_maximum_fusion.2, s32[256,32]{0,1:T(8,128)S(1)} %iota.18), dimensions={1}, to_apply=%region_5.5 | sort | flops 106496 | bytes 131072 | tf_op jit(solution)/shard_map/while/body/eval_jaxpr/jit(sort)/sort | solution.py:29
  76.8 1.1 %sort.36 = (f32[256,32]{0,1:T(8,128)S(1)}, s32[256,32]{0,1:T(8,128)}) sort(f32[256,32]{0,1:T(8,128)S(1)} %pad_maximum_fusion.2, s32[256,32]{0,1:T(8,128)S(1)} %iota.18), dimensions={1}, to_apply=%region_5.5 | sort | flops 106496 | bytes 131072 | tf_op jit(solution)/shard_map/while/body/eval_jaxpr/jit(sort)/sort | solution.py:29
  77.9 0.6 broadcast_multiply_fusion
  (46 shorter events, 0.3 us)
Async XLA Ops:
  7.2 37.4 %reduce-scatter.2.cloned.1.call-start = ((), (), s32[]{:S(2)}) async-start(), calls=%async_computation.1 | async-start | bytes 1310720 | tf_op jit(solution)/shard_map/reduce_scatter | solution.py:61
  14.4 0.7 copy-start
  14.4 0.7 copy-start.5
  14.4 0.7 copy-start.6
  14.4 0.7 copy-start.1
  15.1 44.5 %copy-start.2 = (f32[256]{0:T(256)S(1)}, f32[256]{0:T(256)}, u32[]{:S(2)}) copy-start(f32[256]{0:T(256)} %param.25) | copy-start | bytes 3076
  15.2 44.5 %copy-start.3 = (f32[256]{0:T(256)S(1)}, f32[256]{0:T(256)}, u32[]{:S(2)}) copy-start(f32[256]{0:T(256)} %param.24) | copy-start | bytes 3076
  15.2 44.5 %copy-start.4 = (f32[256]{0:T(256)S(1)}, f32[256]{0:T(256)}, u32[]{:S(2)}) copy-start(f32[256]{0:T(256)} %param.23) | copy-start | bytes 3076
Sparse Core Ops, SparseCore 0:
  14.6 29.9 reduce-scatter.1
where the time goes:
time: 85.7 us; the launch traced here: 85.3 us
  waiting for transfers between devices  29.4 us (34%)
  blocking collectives  21.5 us (25%)
  between operations  14.1 us (16%)
  other arithmetic  12.1 us (14%)
  matrix products  6.14 us (7%)
  local copies, waits for them, and re-layouts  1.82 us (2%)
    reduce_scatter x1, waiting for transfers between devices, on_device(): lax.psum_scatter(lax.dot_general(weights, ceded_loss, contract, preferred...  29.4 us
    psum x1, blocking collectives, on_device(): summed = lax.psum(jnp.sum(kept_annual, axis=1), 'year')  13.2 us
    sort x8, other arithmetic, top_years(): return jnp.sort(values, axis=1)[:, values.shape[1] - keep_count:]  8.77 us
    all_gather x1, blocking collectives, combined_all(): gathered = lax.all_gather(part, axis)  8.27 us
    dot_general x1, matrix products, on_device(): lax.dot_general(weights, ceded_loss, contract, preferred_element_type=jnp...  5.45 us
    min x2, other arithmetic, clamp_between(): return jnp.minimum(jnp.maximum(values, lower), upper)  1.78 us
  transfers between devices with their start and end apart: 1, of which 1 were waited for; matrix products, arithmetic and copies ran while one was open for 0% of the time, Pallas kernels for 0%

commit v1 on v0

--- a/solution.py
+++ b/solution.py
@@ -88,7 +88,7 @@
         - reinstate_rate[:, None] * jnp.minimum(layer_paid, (reinstated * limit_loss)[:, None])
     ) / limit_loss[:, None]
     year_total = YEAR_DEV * lax.axis_size("year")
-    summed = lax.psum(jnp.sum(kept_annual, axis=1), "year")
+    summed = jnp.sum(lax.all_gather(jnp.sum(kept_annual, axis=1), "year"), axis=0)
     base_loss = UNIT_LOSS + summed / year_total
     loss_ratio = kept_annual / base_loss[:, None]
 

time: 85.7 us -> 82.3 us (0.960)
  blocking collectives: 21.5 us -> 18.1 us
    psum x1 -> x0, blocking collectives: 13.2 us -> none  [on_device(): summed = lax.psum(jnp.sum(kept_annual, axis=1), 'year')]
    all_gather x0 -> x1, blocking collectives: none -> 8.9 us  [on_device(): lax.all_gather(jnp.sum(kept_annual, axis=1), 'year')]
    all_gather x1, blocking collectives: 8.27 us -> 9.17 us  [combined_all(): gathered = lax.all_gather(part, axis)]
where the time goes in v1:
time: 82.3 us; the launch traced here: 81.9 us
  waiting for transfers between devices  29.4 us (36%)
  blocking collectives  18.1 us (22%)
  between operations  14.1 us (17%)
  other arithmetic  12.1 us (15%)
  matrix products  6.14 us (7%)
  local copies, waits for them, and re-layouts  1.82 us (2%)
    reduce_scatter x1, waiting for transfers between devices, on_device(): lax.psum_scatter(lax.dot_general(weights, ceded_loss, contract, preferred...  29.4 us
    all_gather x1, blocking collectives, combined_all(): gathered = lax.all_gather(part, axis)  9.17 us
    all_gather x1, blocking collectives, on_device(): lax.all_gather(jnp.sum(kept_annual, axis=1), 'year')  8.9 us
    sort x8, other arithmetic, top_years(): return jnp.sort(values, axis=1)[:, values.shape[1] - keep_count:]  8.77 us
    dot_general x1, matrix products, on_device(): lax.dot_general(weights, ceded_loss, contract, preferred_element_type=jnp...  5.45 us
    min x2, other arithmetic, clamp_between(): return jnp.minimum(jnp.maximum(values, lower), upper)  1.78 us
  transfers between devices with their start and end apart: 1, of which 1 were waited for; matrix products, arithmetic and copies ran while one was open for 0% of the time, Pallas kernels for 0%

profile of v1, /device:TPU:0, one launch (start us, length us, event | category | flops | bytes accessed | tf_op | source)
XLA Modules:
  0.0 81.9 jit_solution(17365447736727325406)
XLA Ops:
  7.2 0.0 reduce-scatter.2.cloned.1.call-start
  7.2 0.9 %fusion.23 = (s32[1024,1]{0,1:T(1,128)S(1)}, s32[1024,1]{0,1:T(1,128)S(1)}, s32[1024,1]{0,1:T(1,128)S(1)}, s32[1024,1]{0,1:T(1,128)S(1)}) fusion(s32[1024,4]{0,1:T(4,128)} %param.19), kind=kLoop, calls=%fused_computation.49 | loop fusion | bytes 32768 | tf_op jit(solution)/shard_map/slice | solution.py:53
  8.1 0.9 %slice_convert_fusion.3 = (f32[1024,1]{0,1:T(1,128)S(1)}, f32[1024,1]{0,1:T(1,128)S(1)}, f32[1024,1]{0,1:T(1,128)S(1)}, f32[1024,1]{0,1:T(1,128)S(1)}) fusion(bf16[1024,4]{0,1:T(4,128)(2,1)} %param.18), kind=kLoop, calls=%fused_computation.41 | loop fusion | flops 4096 | bytes 24576 | tf_op jit(solution)/shard_map/jit(_where)/broadcast_in_dim | solution.py:54
  9.0 5.4 %fusion.10 = bf16[1024,512]{1,0:T(8,128)(2,1)} fusion(f32[1024]{0:T(1024)S(1)} %bitcast.28, s32[1024]{0:T(1024)S(1)} %bitcast.24, f32[1024]{0:T(1024)S(1)} %bitcast.29, s32[1024]{0:T(1024)S(1)} %bitcast.25, f32[1024]{0:T(1024)S(1)} %bitcast.27, s32[1024]{0:T(1024)S(1)} %bitcast.23, f32[1024]{0:T(1024)S(1)} %bitcast.26, s32[1024]{0:T(1024)S(1)} %bitcast.22, ...), kind=kOutput, calls=%fused_computation.19 | convolution fusion | flops 1089994752 | bytes 2138112 | tf_op jit(solution)/shard_map/dot_general | solution.py:62
  14.4 0.0 copy-start
  14.4 0.0 copy-start.5
  14.4 0.0 copy-start.6
  14.4 0.0 copy-start.1
  14.4 0.0 reduce-scatter.2.cloned.1.call-update
  14.5 0.6 copy-done
  15.1 0.0 copy-done.5
  15.1 0.0 copy-done.6
  15.1 0.0 copy-done.1
  15.1 0.0 copy-start.2
  15.2 0.0 copy-start.3
  15.2 0.0 copy-start.4
  15.2 29.4 %reduce-scatter.2.cloned.1.call-done = bf16[256,512]{1,0:T(8,128)(2,1)} async-done(((bf16[1024,512]{1,0:T(8,128)(2,1)}), bf16[256,512]{1,0:T(8,128)(2,1)}) %reduce-scatter.2.cloned.1.call-update) | async-done | bytes 262160 | tf_op jit(solution)/shard_map/reduce_scatter | solution.py:61
  44.6 1.1 %fusion.19 = (f32[256,512]{1,0:T(8,128)S(1)}, f32[256,512]{1,0:T(8,128)S(1)}) fusion(bf16[256,512]{1,0:T(8,128)(2,1)} %reduce-scatter.2.cloned.1.call-done, f32[256]{0:T(256)S(1)} %convert_element_type.35, f32[256]{0:T(256)S(1)} %convert_element_type.34), kind=kLoop, calls=%fused_computation.30 | loop fusion | flops 655360 | bytes 1312768 | tf_op jit(solution)/shard_map/min | solution.py:25
  45.8 0.7 fusion.11
  46.5 8.9 %all-gather.2 = f32[8,1,256]{2,1,0:T(1,128)S(1)} all-gather(f32[1,1,256]{2,1,0:T(1,128)S(1)} %bitcast.21), channel_id=2, replica_groups=mesh['year'=8,'port'=4] {'year'}, dimensions={0}, use_global_device_ids=true | all-gather | bytes 9216 | tf_op jit(solution)/shard_map/all_gather | solution.py:91
  55.4 0.0 copy-done.2
  55.4 0.0 copy-done.3
  55.4 0.0 copy-done.4
  55.4 0.6 maximum_minimum_fusion
  56.1 1.1 %sort.34 = (f32[256,32]{0,1:T(8,128)S(1)}, s32[256,32]{0,1:T(8,128)}) sort(f32[256,32]{0,1:T(8,128)S(1)} %get-tuple-element.110, s32[256,32]{0,1:T(8,128)S(1)} %iota.16), dimensions={1}, to_apply=%region_3.4 | sort | flops 106496 | bytes 131072 | tf_op jit(solution)/shard_map/jit(sort)/sort | solution.py:29
  57.2 9.2 %all-gather.1 = f32[2048,16]{0,1:T(8,128)S(1)} all-gather(f32[256,16]{0,1:T(8,128)S(1)} %slice.54), channel_id=3, replica_groups=mesh['year'=8,'port'=4] {'year'}, dimensions={0}, use_global_device_ids=true | all-gather | bytes 147456 | tf_op jit(solution)/shard_map/all_gather | solution.py:14
  66.4 8.1 %while.15 = (s32[]{:T(128)}, f32[256,16]{0,1:T(8,128)S(1)}, f32[8,256,16]{1,0,2:T(8,128)S(1)}, s32[]{:T(128)}, s32[]{:T(128)}, /*index=5*/s32[]{:T(128)}) while((s32[]{:T(128)}, f32[256,16]{0,1:T(8,128)S(1)}, f32[8,256,16]{1,0,2:T(8,128)S(1)}, s32[]{:T(128)}, s32[]{:T(128)}, /*index=5*/s32[]{:T(128)}) %tuple.57), condition=%wide.region_6.7_spmd, body=%wide.region_4.6_spmd.sunk | while | flops 114693 | bytes 327795 | solution.py:19
  66.5 1.1 %sort.36 = (f32[256,32]{0,1:T(8,128)S(1)}, s32[256,32]{0,1:T(8,128)}) sort(f32[256,32]{0,1:T(8,128)S(1)} %pad_maximum_fusion.2, s32[256,32]{0,1:T(8,128)S(1)} %iota.18), dimensions={1}, to_apply=%region_5.5 | sort | flops 106496 | bytes 131072 | tf_op jit(solution)/shard_map/while/body/eval_jaxpr/jit(sort)/sort | solution.py:29
  67.6 1.1 %sort.36 = (f32[256,32]{0,1:T(8,128)S(1)}, s32[256,32]{0,1:T(8,128)}) sort(f32[256,32]{0,1:T(8,128)S(1)} %pad_maximum_fusion.2, s32[256,32]{0,1:T(8,128)S(1)} %iota.18), dimensions={1}, to_apply=%region_5.5 | sort | flops 106496 | bytes 131072 | tf_op jit(solution)/shard_map/while/body/eval_jaxpr/jit(sort)/sort | solution.py:29
  68.8 1.1 %sort.36 = (f32[256,32]{0,1:T(8,128)S(1)}, s32[256,32]{0,1:T(8,128)}) sort(f32[256,32]{0,1:T(8,128)S(1)} %pad_maximum_fusion.2, s32[256,32]{0,1:T(8,128)S(1)} %iota.18), dimensions={1}, to_apply=%region_5.5 | sort | flops 106496 | bytes 131072 | tf_op jit(solution)/shard_map/while/body/eval_jaxpr/jit(sort)/sort | solution.py:29
  69.9 1.1 %sort.36 = (f32[256,32]{0,1:T(8,128)S(1)}, s32[256,32]{0,1:T(8,128)}) sort(f32[256,32]{0,1:T(8,128)S(1)} %pad_maximum_fusion.2, s32[256,32]{0,1:T(8,128)S(1)} %iota.18), dimensions={1}, to_apply=%region_5.5 | sort | flops 106496 | bytes 131072 | tf_op jit(solution)/shard_map/while/body/eval_jaxpr/jit(sort)/sort | solution.py:29
  71.1 1.1 %sort.36 = (f32[256,32]{0,1:T(8,128)S(1)}, s32[256,32]{0,1:T(8,128)}) sort(f32[256,32]{0,1:T(8,128)S(1)} %pad_maximum_fusion.2, s32[256,32]{0,1:T(8,128)S(1)} %iota.18), dimensions={1}, to_apply=%region_5.5 | sort | flops 106496 | bytes 131072 | tf_op jit(solution)/shard_map/while/body/eval_jaxpr/jit(sort)/sort | solution.py:29
  72.2 1.1 %sort.36 = (f32[256,32]{0,1:T(8,128)S(1)}, s32[256,32]{0,1:T(8,128)}) sort(f32[256,32]{0,1:T(8,128)S(1)} %pad_maximum_fusion.2, s32[256,32]{0,1:T(8,128)S(1)} %iota.18), dimensions={1}, to_apply=%region_5.5 | sort | flops 106496 | bytes 131072 | tf_op jit(solution)/shard_map/while/body/eval_jaxpr/jit(sort)/sort | solution.py:29
  73.4 1.1 %sort.36 = (f32[256,32]{0,1:T(8,128)S(1)}, s32[256,32]{0,1:T(8,128)}) sort(f32[256,32]{0,1:T(8,128)S(1)} %pad_maximum_fusion.2, s32[256,32]{0,1:T(8,128)S(1)} %iota.18), dimensions={1}, to_apply=%region_5.5 | sort | flops 106496 | bytes 131072 | tf_op jit(solution)/shard_map/while/body/eval_jaxpr/jit(sort)/sort | solution.py:29
  74.5 0.6 broadcast_multiply_fusion
  (47 shorter events, 0.4 us)
Async XLA Ops:
  7.2 37.4 %reduce-scatter.2.cloned.1.call-start = ((), (), s32[]{:S(2)}) async-start(), calls=%async_computation.1 | async-start | bytes 1310720 | tf_op jit(solution)/shard_map/reduce_scatter | solution.py:61
  14.4 0.7 copy-start
  14.4 0.7 copy-start.5
  14.4 0.7 copy-start.6
  14.4 0.7 copy-start.1
  15.1 40.3 %copy-start.2 = (f32[256]{0:T(256)S(1)}, f32[256]{0:T(256)}, u32[]{:S(2)}) copy-start(f32[256]{0:T(256)} %param.25) | copy-start | bytes 3076
  15.2 40.3 %copy-start.3 = (f32[256]{0:T(256)S(1)}, f32[256]{0:T(256)}, u32[]{:S(2)}) copy-start(f32[256]{0:T(256)} %param.24) | copy-start | bytes 3076
  15.2 40.3 %copy-start.4 = (f32[256]{0:T(256)S(1)}, f32[256]{0:T(256)}, u32[]{:S(2)}) copy-start(f32[256]{0:T(256)} %param.23) | copy-start | bytes 3076
Sparse Core Ops, SparseCore 0:
  14.6 29.9 reduce-scatter.1
